TPU v7x, 512 devices: a whole 4x4x16 slice. The times are simulated.
512 devices in a mesh: grp: 8 (over x, core), wide: 64 (over y, z).
Axes of the slice: x: 4, y: 4, z: 16, core: 2. Of those that a mesh axis runs over, the one named last changes fastest.
Arguments:
- cluster_coefficients: bfloat16 [512, 24576], P(('grp', 'wide')), may hold values from -6 to 6
- exchange_repulsion_matrix: bfloat16 [512, 24576], P(('grp', 'wide')), may hold values from -6 to 6
- quadruple_virtual_tensor: bfloat16 [24576, 24576], P('grp', 'wide'), may hold values from -0.0546875 to 0.0546875
- retained_submatrix_flags: int32 [384, 384], P('grp', 'wide'), may hold values 0 or 1
- front_group_coupling_matrix: float32 [6, 64, 64], replicated, may hold values from -0.6 to 0.6
- rear_group_coupling_matrix: float32 [6, 64, 64], replicated, may hold values from -0.6 to 0.6
- hole_level_sums: float32 [512], P(('grp', 'wide')), may hold values from -2 to -0.5
- particle_level_sums: float32 [24576], replicated, may hold values from 0.5 to 4
Outputs:
- increment: float32 [512, 24576], P(('grp', 'wide'))
All inputs are finite; a program needn't handle non-finite values. No bound on the sum of `retained_submatrix_flags` on one device may be relied on, other than what follows from the above.
Results may differ from a plain program's by a relative error of at most 0.0003.
Values may be sent and summed in bfloat16 or wider, within the bound.
A program may use at most 64 MiB of HBM per device.

v0:
```python
import jax
import jax.numpy as jnp
from jax import lax
from jax.sharding import PartitionSpec as P


def fock_terms(cluster_coefficients, front_group_coupling_matrix, rear_group_coupling_matrix):
    row_count, full_width = cluster_coefficients.shape
    tile_pairs = front_group_coupling_matrix.shape[0]
    group_width_value = front_group_coupling_matrix.shape[1]
    local_amplitude_block = cluster_coefficients.astype(jnp.float32).reshape(
        row_count, tile_pairs, group_width_value, group_width_value
    )
    leading_term = jnp.einsum(
        "khd,jkdw->jkhw",
        front_group_coupling_matrix,
        local_amplitude_block,
        precision=lax.Precision.HIGHEST,
    )
    second_term = jnp.einsum(
        "tbd,ptad->ptab",
        rear_group_coupling_matrix,
        local_amplitude_block,
        precision=lax.Precision.HIGHEST,
    )
    return (leading_term + second_term).reshape(row_count, full_width)


def prune_submatrix(quadruple_virtual_tensor, retained_submatrix_flags, group_width_value):
    cd_rows, ab_cols = quadruple_virtual_tensor.shape
    kept_column_flags = jnp.repeat(retained_submatrix_flags, group_width_value, axis=1).astype(
        jnp.bfloat16
    )
    shaped = quadruple_virtual_tensor.reshape(
        cd_rows // group_width_value, group_width_value, ab_cols
    )
    return (shaped * kept_column_flags[:, None, :]).reshape(cd_rows, ab_cols)


def local(
    cluster_coefficients,
    exchange_repulsion_matrix,
    quadruple_virtual_tensor,
    retained_submatrix_flags,
    front_group_coupling_matrix,
    rear_group_coupling_matrix,
    hole_level_sums,
    particle_level_sums,
):
    group_width_value = front_group_coupling_matrix.shape[1]
    pruned_particle_contraction = prune_submatrix(
        quadruple_virtual_tensor, retained_submatrix_flags, group_width_value
    )
    fock_term = fock_terms(
        cluster_coefficients, front_group_coupling_matrix, rear_group_coupling_matrix
    )
    gathered = lax.all_gather(cluster_coefficients, "wide", axis=0, tiled=True)
    regrouped = lax.all_to_all(gathered, "grp", split_axis=1, concat_axis=0, tiled=True)
    partial_contribution = jnp.dot(
        regrouped, pruned_particle_contraction, preferred_element_type=jnp.float32
    )
    summed = lax.psum_scatter(partial_contribution, "grp", scatter_dimension=0, tiled=True)
    returned = lax.all_to_all(summed, "wide", split_axis=0, concat_axis=1, tiled=True)
    residual = exchange_repulsion_matrix.astype(jnp.float32) + fock_term + returned
    return residual / (particle_level_sums[None, :] - hole_level_sums[:, None])


def solution(mesh):
    return jax.shard_map(
        local,
        mesh=mesh,
        in_specs=(
            P(("grp", "wide"), None),
            P(("grp", "wide"), None),
            P("grp", "wide"),
            P("grp", "wide"),
            P(),
            P(),
            P(("grp", "wide")),
            P(),
        ),
        out_specs=P(("grp", "wide"), None),
        check_vma=False,
    )
```

profile of v0, /device:TPU:1, one launch (start us, length us, event | category | flops | bytes accessed | tf_op | source)
XLA Modules:
  0.0 304.8 jit_solution(10158778777224716283)
XLA Ops:
  6.5 0.0 copy-start
  6.5 0.0 all-gather.3.cloned.1.call-start
  6.5 0.7 all-gather.3.cloned.1.call-update
  7.3 151.0 %all-gather.3.cloned.1.call-done = bf16[64,1,24576]{2,1,0:T(2,128)(2,1)} async-done(((bf16[1,1,24576]{2,1,0:T(2,128)(2,1)}), bf16[64,1,24576]{2,1,0:T(2,128)(2,1)}) %all-gather.3.cloned.1.call-update) | async-done | bytes 3145744 | tf_op jit(solution)/shard_map/all_gather | solution.py:57
  158.3 18.3 %reduce.1 = bf16[64,24576]{1,0:T(8,128)(2,1)S(1)} reduce(bf16[64,1,24576]{2,1,0:T(2,128)(2,1)} %all-gather.3.cloned.1.call-done, bf16[]{:T(256)} %constant.4), dimensions={1}, to_apply=%all-gather.reduce_sub_computation | reduce | bytes 6291458 | tf_op jit(solution)/shard_map/all_gather | solution.py:57
  176.6 1.9 copy.30
  178.5 13.1 %all-to-all-start = ((bf16[64,8,3072]{2,0,1:T(8,128)(2,1)}), bf16[64,8,3072]{2,0,1:T(8,128)(2,1)S(1)}, u32[]{:S(2)}, u32[]{:S(2)}) async-start(bf16[64,8,3072]{2,0,1:T(8,128)(2,1)} %bitcast.32), calls=%async_computation | async-start | bytes 6291456 | tf_op jit(solution)/shard_map/all_to_all | solution.py:58
  191.6 0.0 reduce-scatter.4.cloned.1.call-start
  191.6 0.0 copy-done.5
  191.6 0.1 copy.21
  191.7 0.1 broadcast_in_dim.2
  191.8 0.1 convert_element_type.17
  192.0 3.4 %bitcast_multiply_fusion = bf16[3072,384]{1,0:T(8,128)(2,1)} fusion(bf16[3072,384]{1,0:T(8,128)(2,1)} %param.10, bf16[48,384]{1,0:T(8,128)(2,1)S(1)} %convert_element_type.17), kind=kLoop, calls=%fused_computation.1 | loop fusion | flops 1179648 | bytes 4755456 | tf_op jit(solution)/shard_map/mul | solution.py:37
  195.3 33.7 %all-to-all-done = bf16[64,8,3072]{2,0,1:T(8,128)(2,1)S(1)} async-done(((bf16[64,8,3072]{2,0,1:T(8,128)(2,1)}), bf16[64,8,3072]{2,0,1:T(8,128)(2,1)S(1)}, u32[]{:S(2)}, u32[]{:S(2)}) %all-to-all-start) | async-done | bytes 3145760 | tf_op jit(solution)/shard_map/all_to_all | solution.py:58
  229.0 4.0 %convolution_bitcast_fusion = f32[512,384]{0,1:T(8,128)} fusion(bf16[3072,384]{1,0:T(8,128)(2,1)} %bitcast_multiply_fusion, bf16[512,3072]{1,0:T(8,128)(2,1)S(1)} %bitcast.35), kind=kOutput, calls=%fused_computation.2 | convolution fusion | flops 1207959552 | bytes 6291456 | tf_op jit(solution)/shard_map/dot_general | solution.py:59
  233.0 2.3 copy.26
  235.4 0.0 reduce-scatter.4.cloned.1.call-update
  235.4 0.0 copy-done.1
  235.4 0.3 reduce
  236.3 0.1 reshape.36
  236.4 0.0 copy-done
  236.4 0.3 convolution_bitcast_fusion.1
  236.7 0.0 copy-done.2
  236.7 0.3 fusion
  237.1 0.1 copy.20
  237.2 0.2 reshape.37
  237.3 29.9 %reduce-scatter.4.cloned.1.call-done = f32[64,384]{1,0:T(8,128)} async-done(((f32[512,384]{1,0:T(8,128)}), f32[64,384]{1,0:T(8,128)}) %reduce-scatter.4.cloned.1.call-update) | async-done | bytes 98320
  267.2 1.0 copy.27
  268.3 0.8 copy.23
  269.0 14.4 %all-to-all-start.1 = ((f32[64,1,384]{2,1,0:T(1,128)}), f32[64,1,384]{2,1,0:T(1,128)S(1)}, u32[]{:S(2)}, u32[]{:S(2)}) async-start(f32[64,1,384]{2,1,0:T(1,128)} %copy.23), calls=%async_computation.1 | async-start | bytes 196608 | tf_op jit(solution)/shard_map/all_to_all | solution.py:63
  283.4 13.7 %all-to-all-done.1 = f32[64,1,384]{2,1,0:T(1,128)S(1)} async-done(((f32[64,1,384]{2,1,0:T(1,128)}), f32[64,1,384]{2,1,0:T(1,128)S(1)}, u32[]{:S(2)}, u32[]{:S(2)}) %all-to-all-start.1) | async-done | bytes 98336 | tf_op jit(solution)/shard_map/all_to_all | solution.py:63
  297.1 0.8 add_divide_fusion
  (9 shorter events, 0.0 us)
Async XLA Ops:
  6.5 229.9 %copy-start = (f32[6,64,64]{2,1,0:T(8,128)S(1)}, f32[6,64,64]{2,1,0:T(8,128)}, u32[]{:S(2)}) copy-start(f32[6,64,64]{2,1,0:T(8,128)} %param.13) | copy-start | bytes 294916
  6.5 151.7 %all-gather.3.cloned.1.call-start = ((), (), s32[]{:S(2)}) async-start(), calls=%async_computation.3 | async-start | bytes 6389760 | tf_op jit(solution)/shard_map/all_gather | solution.py:57
  178.5 13.1 %copy-start.5 = (s32[48,6]{0,1:T(8,128)S(1)}, s32[48,6]{0,1:T(8,128)}, u32[]{:S(2)}) copy-start(s32[48,6]{0,1:T(8,128)} %param.11) | copy-start | bytes 3460
  178.5 50.5 %all-to-all-start = ((bf16[64,8,3072]{2,0,1:T(8,128)(2,1)}), bf16[64,8,3072]{2,0,1:T(8,128)(2,1)S(1)}, u32[]{:S(2)}, u32[]{:S(2)}) async-start(bf16[64,8,3072]{2,0,1:T(8,128)(2,1)} %bitcast.32), calls=%async_computation | async-start | bytes 6291456 | tf_op jit(solution)/shard_map/all_to_all | solution.py:58
  191.6 75.7 %reduce-scatter.4.cloned.1.call-start = ((), (), s32[]{:S(2)}) async-start(), calls=%async_computation.4 | async-start | bytes 884736
  233.0 2.4 copy-start.1
  233.0 3.7 %copy-start.2 = (f32[6,64,64]{2,1,0:T(8,128)S(1)}, f32[6,64,64]{2,1,0:T(8,128)}, u32[]{:S(2)}) copy-start(f32[6,64,64]{2,1,0:T(8,128)} %param.12) | copy-start | bytes 294916
  233.0 50.4 %copy-start.3 = (f32[24576]{0:T(1024)S(1)}, f32[24576]{0:T(1024)}, u32[]{:S(2)}) copy-start(f32[24576]{0:T(1024)} %param.15) | copy-start | bytes 294916
  235.4 61.8 %copy-start.4 = (bf16[1,24576]{1,0:T(2,128)(2,1)S(1)}, bf16[1,24576]{1,0:T(2,128)(2,1)}, u32[]{:S(2)}) copy-start(bf16[1,24576]{1,0:T(2,128)(2,1)} %param.9) | copy-start | bytes 147460
  269.0 28.1 %all-to-all-start.1 = ((f32[64,1,384]{2,1,0:T(1,128)}), f32[64,1,384]{2,1,0:T(1,128)S(1)}, u32[]{:S(2)}, u32[]{:S(2)}) async-start(f32[64,1,384]{2,1,0:T(1,128)} %copy.23), calls=%async_computation.1 | async-start | bytes 196608 | tf_op jit(solution)/shard_map/all_to_all | solution.py:63
Sparse Core Ops, SparseCore 0:
  10.3 147.9 all-gather.2
  235.5 31.6 reduce-scatter.3
where the time goes:
time: 307 us; the launch traced here: 305 us
  waiting for transfers between devices  229 us (75%)
  starting transfers between devices  27.5 us (9%)
  other arithmetic  22.8 us (7%)
  between operations  14.2 us (5%)
  local copies, waits for them, and re-layouts  6.77 us (2%)
  matrix products  4.61 us (2%)
    all_gather x1, waiting for transfers between devices, local(): gathered = lax.all_gather(cluster_coefficients, 'wide', axis=0, tiled=True)  151 us
    all_to_all x1, waiting for transfers between devices, local(): lax.all_to_all(gathered, 'grp', split_axis=1, concat_axis=0, tiled=True)  33.7 us
    unnamed x3, waiting for transfers between devices  30.6 us
    all_gather x1, other arithmetic, local(): gathered = lax.all_gather(cluster_coefficients, 'wide', axis=0, tiled=True)  18.3 us
    all_to_all x1, starting transfers between devices, local(): lax.all_to_all(summed, 'wide', split_axis=0, concat_axis=1, tiled=True)  14.4 us
    all_to_all x1, waiting for transfers between devices, local(): lax.all_to_all(summed, 'wide', split_axis=0, concat_axis=1, tiled=True)  13.7 us
    all_to_all x1, starting transfers between devices, local(): lax.all_to_all(gathered, 'grp', split_axis=1, concat_axis=0, tiled=True)  13.1 us
  transfers between devices with their start and end apart: 4, of which 4 were waited for; matrix products, arithmetic and copies ran while one was open for 2% of the time, Pallas kernels for 0%

commit v1 on v0

v1 whole, which is shorter than its diff:
```python
import jax
import jax.numpy as jnp
from jax import lax
from jax.experimental import pallas as pl
from jax.experimental.pallas import tpu as pltpu
from jax.sharding import PartitionSpec as P

MESH = pl.DeviceIdType.MESH
F32 = jnp.float32
BF16 = jnp.bfloat16

NG = 8
NY = 4
NZ = 16
NW = 64
KG = 3072
KH = 1536
KA = 512
KB = 1024
Q = 384
NQ = 192


def kernel(
    t_hbm, e_hbm, v_hbm, fl_hbm, f_hbm, r_hbm, hls, pls_hbm,
    out,
    trow, erow, vbuf, fl, mask, fbuf, rbuf, pls, tnat, base, inv,
    asrc, arecv, ta, tb, obuf, sbuf, xr, fs, lad,
    ld_sem, a_send, a_recv, ay_recv, az_recv, bz_recv, by_recv, x_recv, l_recv,
    ta_send, tb_send, x_send, l_send,
):
    g = lax.axis_index("grp")
    w = lax.axis_index("wide")
    y = w // NZ
    z = w % NZ

    def wid(yy, zz):
        return lax.rem(yy + 2 * NY, NY) * NZ + lax.rem(zz + 2 * NZ, NZ)

    def rcopy(src, dst, ss, rs, gg, ww):
        return pltpu.make_async_remote_copy(
            src_ref=src, dst_ref=dst, send_sem=ss, recv_sem=rs,
            device_id=(gg, ww), device_id_type=MESH,
        )

    loads = [
        pltpu.make_async_copy(s, d, ld_sem.at[i])
        for i, (s, d) in enumerate([
            (t_hbm, trow), (fl_hbm, fl), (v_hbm, vbuf), (f_hbm, fbuf),
            (r_hbm, rbuf), (e_hbm, erow), (pls_hbm, pls),
        ])
    ]
    for c in loads:
        c.start()

    barrier = pltpu.get_barrier_semaphore()
    for d in range(1, NG):
        pl.semaphore_signal(barrier, inc=1, device_id=(lax.rem(g + d, NG), w), device_id_type=MESH)
    for ww in (wid(y + 1, z), wid(y - 1, z), wid(y + 2, z), wid(y, z + 1), wid(y, z - 1)):
        pl.semaphore_signal(barrier, inc=1, device_id=(g, ww), device_id_type=MESH)

    loads[0].wait()
    row = trow[...].astype(F32)
    for d in range(NG):
        asrc[d] = row[:, d * KG:(d + 1) * KG]
    pl.semaphore_wait(barrier, NG - 1 + 5)

    for d in range(1, NG):
        gg = lax.rem(g + d, NG)
        rcopy(asrc.at[gg], arecv.at[g], a_send, a_recv, gg, w).start()
    arecv[g] = asrc[g]

    loads[1].wait()
    qi = lax.broadcasted_iota(jnp.int32, (6, Q), 1) // 64
    onehot = jnp.where(qi == lax.broadcasted_iota(jnp.int32, (6, Q), 0), 1.0, 0.0).astype(F32)
    mask[...] = lax.dot_general(
        fl[...].astype(F32), onehot, (((0,), (0,)), ((), ())), preferred_element_type=F32
    )
    rcopy(asrc.at[pl.ds(0, NG - 1)], arecv.at[pl.ds(0, NG - 1)], a_send, a_recv, g, w).wait_recv()

    for gg in range(NG):
        tnat[pl.ds(gg, 1), :] = arecv[gg]
    lo, hi = tnat[:, :KH], tnat[:, KH:]
    ta[w] = jnp.concatenate([lo[:, :KA], hi[:, :KA]], axis=0).astype(BF16)
    tb[w] = jnp.concatenate([lo[:, KA:], hi[:, KA:]], axis=0).astype(BF16)

    zp, zm = wid(y, z + 1), wid(y, z - 1)
    yp, ym, y2 = wid(y + 1, z), wid(y - 1, z), wid(y + 2, z)
    zn = (zp, zm)

    def send_a(blk, ww, rs):
        rcopy(ta.at[blk], ta.at[blk], ta_send, rs, g, ww).start()

    def send_b(blk, ww, rs):
        rcopy(tb.at[blk], tb.at[blk], tb_send, rs, g, ww).start()

    def wait_a(blk, rs):
        rcopy(ta.at[blk], ta.at[blk], ta_send, rs, g, w).wait_recv()

    def wait_b(blk, rs):
        rcopy(tb.at[blk], tb.at[blk], tb_send, rs, g, w).wait_recv()

    send_a(w, yp, ay_recv.at[0])
    send_a(w, ym, ay_recv.at[1])
    send_a(w, y2, ay_recv.at[2])
    for d in range(2):
        send_b(w, zn[d], bz_recv.at[d, 1])
        send_a(w, zn[d], az_recv.at[d, 1, 0])
    send_b(w, yp, by_recv.at[0, 1, 0])
    send_b(w, ym, by_recv.at[0, 1, 1])

    loads[2].wait()

    def screen(i, _):
        m = mask[pl.ds(i, 1), :].astype(BF16)
        rows = pl.ds(pl.multiple_of(i * 64, 64), 64)
        vbuf[rows, :] = vbuf[rows, :] * m
        return 0

    lax.fori_loop(0, 48, screen, 0)

    for slot, dy in ((0, 3), (1, 1), (2, 2)):
        blk = wid(y + dy, z)
        wait_a(blk, ay_recv.at[slot])
        for d in range(2):
            send_a(blk, zn[d], az_recv.at[d, 1, dy])

    for c in loads[3:]:
        c.wait()

    def fock(t, _):
        rows = pl.ds(pl.multiple_of(t * 32, 32), 32)
        for k in range(32):
            o = pl.multiple_of(t * 4096 + k * 128, 128)
            base[pl.ds(t * 32 + k, 1), :] = trow[:, pl.ds(o, 128)].astype(F32)
        x = base[rows, :]
        xr_ = jnp.concatenate([x[:, :64], x[:, 64:]], axis=0).astype(BF16)
        i0 = lax.broadcasted_iota(jnp.int32, (64, 64), 0)
        i1 = lax.broadcasted_iota(jnp.int32, (64, 64), 1)
        perm = jnp.where(i1 == lax.rem(i0, 32) * 2 + i0 // 32, 1.0, 0.0).astype(BF16)
        dn = (((1,), (0,)), ((), ()))
        dt = (((1,), (1,)), ((), ()))
        dl = (((0,), (0,)), ((), ()))
        f = fbuf[t]
        fh = f.astype(BF16)
        fl_ = (f - fh.astype(F32)).astype(BF16)
        r = rbuf[t]
        rh = r.astype(BF16)
        rl = (r - rh.astype(F32)).astype(BF16)
        dot = lambda a, b, d: lax.dot_general(a, b, d, preferred_element_type=F32)
        c = dot(perm, xr_, dl).astype(BF16)
        fph = dot(perm, fh, dn).astype(BF16)
        fpl = dot(perm, fl_, dn).astype(BF16)
        o = dot(fph, c, dn) + dot(fpl, c, dn) + dot(xr_, rh, dt) + dot(xr_, rl, dt)
        base[rows, :] = jnp.concatenate([o[:32], o[32:]], axis=1)
        return 0

    lax.fori_loop(0, 6, fock, 0)

    h = hls[0]

    def finish_base(k, _):
        o = pl.multiple_of(k * 128, 128)
        lad_b = base[pl.ds(k, 1), :] + erow[:, pl.ds(o, 128)].astype(F32)
        inv[k] = 1.0 / (pls[k] - h)
        base[pl.ds(k, 1), :] = lad_b
        return 0

    lax.fori_loop(0, NQ, finish_base, 0)

    def col(s, d):
        return z - s if d == 0 else z + lax.rem(s, 8)

    def step(i, _):
        @pl.when(i <= 8)
        def _():
            for d in range(2):
                last = 8 - d

                @pl.when(i <= last)
                def _():
                    cz = col(i, d)
                    blk = wid(y, cz)
                    wait_b(blk, bz_recv.at[d, i])

                    @pl.when(i < last)
                    def _():
                        send_b(blk, zn[d], bz_recv.at[d, i + 1])

                    send_b(blk, yp, by_recv.at[i, d, 0])
                    send_b(blk, ym, by_recv.at[i, d, 1])
            for dy in (0, 3, 1, 2):
                for d in range(2):
                    last = 8 - d

                    @pl.when(i <= last)
                    def _():
                        blk = wid(y + dy, col(i, d))
                        wait_a(blk, az_recv.at[d, i, dy])

                        @pl.when(i < last)
                        def _():
                            send_a(blk, zn[d], az_recv.at[d, i + 1, dy])

        s1 = i - 1

        @pl.when((s1 >= 1) & (s1 <= 8))
        def _():
            blk = wid(y - 1, col(s1, 0))
            wait_b(blk, by_recv.at[s1, 0, 0])
            send_b(blk, yp, by_recv.at[s1, 0, 2])

        @pl.when(s1 <= 7)
        def _():
            blk = wid(y + 1, col(s1, 1))
            wait_b(blk, by_recv.at[s1, 1, 1])
            send_b(blk, ym, by_recv.at[s1, 1, 2])

        s2 = i - 2

        @pl.when((s2 >= 1) & (s2 <= 8))
        def _():
            s = s2
            sm = lax.rem(s, 8)
            wait_b(wid(y + 1, col(s, 0)), by_recv.at[s, 0, 1])
            wait_b(wid(y + 2, col(s, 0)), by_recv.at[s, 0, 2])
            wait_b(wid(y - 1, col(s, 1)), by_recv.at[sm, 1, 0])
            wait_b(wid(y + 2, col(s, 1)), by_recv.at[sm, 1, 2])
            blks = [wid(y + dy, col(s, d)) for d in range(2) for dy in range(NY)]
            xa = jnp.concatenate([ta[b] for b in blks], axis=0)
            xb = jnp.concatenate([tb[b] for b in blks], axis=0)
            total = None
            for hh in range(2):
                k0 = hh * KH
                o = jnp.dot(xa, vbuf[k0:k0 + KA, :], preferred_element_type=F32)
                o += jnp.dot(xb, vbuf[k0 + KA:k0 + KH, :], preferred_element_type=F32)
                o = o.reshape(8, 16, Q)[:, 8 * hh:8 * hh + 8, :]
                total = o if total is None else total + o
            total = total.reshape(64, Q)
            for c in range(3):
                obuf[c] = total[:, c * 128:(c + 1) * 128]
            for d in range(NG):
                for c in range(3):
                    sbuf[(s - 1) * NG + d, :, c * 128:(c + 1) * 128] = obuf[c, pl.ds(d, 8, stride=8), :]
            for d in range(1, NG):
                gg = lax.rem(g + d, NG)
                rcopy(sbuf.at[(s - 1) * NG + gg], xr.at[(s - 1) * NG + g], x_send, x_recv.at[s - 1], gg, w).start()
            xr[(s - 1) * NG + g] = sbuf[(s - 1) * NG + g]

        s3 = i - 3

        @pl.when((s3 >= 1) & (s3 <= 8))
        def _():
            s = s3
            win = pl.ds((s - 1) * NG, NG - 1)
            rcopy(sbuf.at[win], xr.at[win], x_send, x_recv.at[s - 1], g, w).wait_recv()
            tot = jnp.sum(xr[pl.ds((s - 1) * NG, NG)], axis=0)
            for n in range(8):
                for c in range(3):
                    fs[(s - 1) * 24 + 3 * n + c] = tot[n:n + 1, c * 128:(c + 1) * 128]
            for d in range(2):
                for dy in range(NY):
                    n = d * NY + dy
                    src = fs.at[pl.ds((s - 1) * 24 + 3 * n, 3)]

                    def push():
                        rcopy(src, lad.at[pl.ds(3 * w, 3)], l_send, l_recv, g, wid(y + dy, col(s, d))).start()

                    if d == 1 and dy == 0:
                        pl.when(s < 8)(push)

                        @pl.when(s == 8)
                        def _():
                            for c in range(3):
                                lad[3 * w + c] = fs[(s - 1) * 24 + 3 * n + c]
                    else:
                        push()
        return 0

    lax.fori_loop(1, 12, step, 0)

    part = pl.ds(0, 3 * (NW - 1))
    rcopy(fs.at[part], lad.at[part], l_send, l_recv, g, w).wait_recv()

    def finish(k, _):
        out[k] = (lad[k] + base[pl.ds(k, 1), :]) * inv[k]
        return 0

    lax.fori_loop(0, NQ, finish, 0)

    rcopy(asrc.at[pl.ds(0, NG - 1)], arecv.at[pl.ds(0, NG - 1)], a_send, a_recv, g, w).wait_send()
    rcopy(ta.at[pl.ds(0, NW - 1)], ta.at[pl.ds(0, NW - 1)], ta_send, ay_recv.at[0], g, w).wait_send()
    rcopy(tb.at[pl.ds(0, NW - 1)], tb.at[pl.ds(0, NW - 1)], tb_send, ay_recv.at[0], g, w).wait_send()
    rcopy(sbuf.at[pl.ds(0, 56)], xr.at[pl.ds(0, 56)], x_send, x_recv.at[0], g, w).wait_send()
    rcopy(fs.at[part], lad.at[part], l_send, l_recv, g, w).wait_send()


def local(t, e, v, flags, f, r, hls, pls):
    any_spec = pl.BlockSpec(memory_space=pl.ANY)
    vm = pltpu.VMEM
    dma = pltpu.SemaphoreType.DMA
    res = pl.pallas_call(
        kernel,
        out_shape=jax.ShapeDtypeStruct((NQ, 1, 128), F32),
        in_specs=[any_spec] * 6 + [pl.BlockSpec(memory_space=pltpu.SMEM), any_spec],
        out_specs=pl.BlockSpec(memory_space=pltpu.VMEM),
        scratch_shapes=[
            vm((1, 24576), BF16),
            vm((1, 24576), BF16),
            vm((KG, Q), BF16),
            vm((6, 48), jnp.int32),
            vm((48, Q), F32),
            vm((6, 64, 64), F32),
            vm((6, 64, 64), F32),
            vm((NQ, 1, 128), F32),
            vm((NG, KG), F32),
            vm((NQ, 128), F32),
            vm((NQ, 1, 128), F32),
            vm((NG, 1, KG), F32),
            vm((NG, 1, KG), F32),
            vm((NW, 16, KA), BF16),
            vm((NW, 16, KB), BF16),
            vm((3, 64, 128), F32),
            vm((64, 8, Q), F32),
            vm((64, 8, Q), F32),
            vm((NQ, 1, 128), F32),
            vm((NQ, 1, 128), F32),
            dma((7,)),
            dma,
            dma,
            dma((3,)),
            dma((2, 9, 4)),
            dma((2, 9)),
            dma((9, 2, 3)),
            dma((8,)),
            dma,
            dma,
            dma,
            dma,
            dma,
        ],
        compiler_params=pltpu.CompilerParams(
            collective_id=0, has_side_effects=True, vmem_limit_bytes=60 * 1024 * 1024
        ),
        name="ladder",
    )(t, e, v, flags.T, f, r, hls, pls.reshape(NQ, 1, 128))
    return res.reshape(1, 24576)


def solution(mesh):
    return jax.shard_map(
        local,
        mesh=mesh,
        in_specs=(
            P(("grp", "wide"), None),
            P(("grp", "wide"), None),
            P("grp", "wide"),
            P("grp", "wide"),
            P(),
            P(),
            P(("grp", "wide")),
            P(),
        ),
        out_specs=P(("grp", "wide"), None),
        check_vma=False,
    )
```

time: 307 us -> 73.8 us (0.24)
  waiting for transfers between devices: 229 us -> 0 us
  Pallas kernels: 0 us -> 71.4 us
  starting transfers between devices: 27.5 us -> 0 us
  other arithmetic: 22.8 us -> 0 us
  between operations: 14.2 us -> 0.66 us
  local copies, waits for them, and re-layouts: 6.77 us -> 1.54 us
  matrix products: 4.61 us -> 0 us
    all_gather x1 -> x0, waiting for transfers between devices: 151 us -> none  [local(): gathered = lax.all_gather(cluster_coefficients, 'wide', axis=0, tiled=True)]
    pallas_call x0 -> x1, Pallas kernels: none -> 71.4 us  [local(): pl.pallas_call(kernel, out_shape=jax.ShapeDtypeStruct((NQ, 1, 128), F32),...]
    all_to_all x2 -> x0, waiting for transfers between devices: 47.4 us -> none  [the longest x1 33.7 us: local(): lax.all_to_all(gathered, 'grp', split_axis=1, concat_axis=0, tiled=True)]
    unnamed x3 -> x0, waiting for transfers between devices: 30.6 us -> none
    all_to_all x2 -> x0, starting transfers between devices: 27.5 us -> none  [the longest x1 14.4 us: local(): lax.all_to_all(summed, 'wide', split_axis=0, concat_axis=1, tiled=True)]
    all_gather x1 -> x0, other arithmetic: 18.3 us -> none  [local(): gathered = lax.all_gather(cluster_coefficients, 'wide', axis=0, tiled=True)]
    dot_general x3 -> x0, matrix products: 4.61 us -> none  [the longest x1 4 us: local(): jnp.dot(regrouped, pruned_particle_contraction, preferred_element_type=jn...]
    mul x1 -> x0, other arithmetic: 3.37 us -> none  [prune_submatrix(): return (shaped * kept_column_flags[:, None, :]).reshape(cd_rows, ab_cols)]
  transfers between devices with their start and end apart: 4 -> 0, of which waited for: 4 -> 0; matrix products, arithmetic and copies ran while one was open for 2% -> 0% of each run, Pallas kernels for 0% -> 0%
where the time goes in v1:
time: 73.8 us; the launch traced here: 73.6 us
  Pallas kernels  71.4 us (97%)
  local copies, waits for them, and re-layouts  1.54 us (2%)
    pallas_call x1, Pallas kernels, local(): pl.pallas_call(kernel, out_shape=jax.ShapeDtypeStruct((NQ, 1, 128), F32),...  71.4 us
    unnamed x1, local copies, waits for them, and re-layouts  1.54 us

profile of v1, /device:TPU:1, one launch (start us, length us, event | category | flops | bytes accessed | tf_op | source)
XLA Modules:
  0.0 73.6 jit_solution(15024527209737980592)
XLA Ops:
  0.7 71.4 %ladder.1 = f32[192,1,128]{2,1,0:T(1,128)} custom-call(bf16[1,24576]{1,0:T(2,128)(2,1)} %t_hbm.1, bf16[1,24576]{1,0:T(2,128)(2,1)} %e_hbm.1, bf16[3072,384]{1,0:T(8,128)(2,1)} %v_hbm.1, s32[6,48]{1,0:T(8,128)} %bitcast.5, f32[6,64,64]{2,1,0:T(8,128)} %f_hbm.1, f32[6,64,64]{2,1,0:T(8,128)} %r_hbm.1, f32[1]{0:T(128)S(6)} %copy.10.hls, f32[192,1,128]{2,1,0:T(1,128)} %bitcast.4), custom_call_target="tpu_custom_call" | custom-call | tf_op jit(solution)/shard_map/ladder/pallas_call | solution.py:302
  72.1 1.5 %copy.11 = f32[1,24576]{1,0:T(1,128)} copy(f32[1,24576]{1,0:T(1,128)} %bitcast.3) | data formatting | bytes 196608

commit v2 on v0

v2 whole, which is shorter than its diff:
```python
import jax
import jax.numpy as jnp
from jax import lax
from jax.experimental import pallas as pl
from jax.experimental.pallas import tpu as pltpu
from jax.sharding import PartitionSpec as P

MESH = pl.DeviceIdType.MESH
F32 = jnp.float32
BF16 = jnp.bfloat16

NG = 8
NY = 4
NZ = 16
NW = 64
KG = 3072
KA = 512
KB = 1024
Q = 384
NQ = 192


def kernel(
    t_hbm, e_hbm, v_hbm, fl_hbm, f_hbm, r_hbm, hls, pls_hbm,
    out,
    trow, erow, vbuf, fl, mask, fbuf, rbuf, pls, tnat, base, base3, inv3,
    tsend, st0, stz, sty, scr, ta, tb, acc, obuf, sbuf, xr, fs, lad,
    ld_sem, s0_recv, sz_recv, sy_recv, az_recv, bz_recv, by_recv, x_recv, l_recv,
    s0_send, sz_send, sy_send, ta_send, tb_send, x_send, l_send,
):
    g = lax.axis_index("grp")
    w = lax.axis_index("wide")
    y = w // NZ
    z = w % NZ

    def wid(yy, zz):
        return lax.rem(yy + 2 * NY, NY) * NZ + lax.rem(zz + 2 * NZ, NZ)

    def rcopy(src, dst, ss, rs, gg, ww):
        return pltpu.make_async_remote_copy(
            src_ref=src, dst_ref=dst, send_sem=ss, recv_sem=rs,
            device_id=(gg, ww), device_id_type=MESH,
        )

    zp, zm = wid(y, z + 1), wid(y, z - 1)
    yp, ym, y2 = wid(y + 1, z), wid(y - 1, z), wid(y + 2, z)
    zn = (zp, zm)

    loads = [
        pltpu.make_async_copy(s, d, ld_sem.at[i])
        for i, (s, d) in enumerate([
            (t_hbm, trow), (fl_hbm, fl), (v_hbm, vbuf), (f_hbm, fbuf),
            (r_hbm, rbuf), (e_hbm, erow), (pls_hbm, pls),
        ])
    ]
    for c in loads:
        c.start()

    barrier = pltpu.get_barrier_semaphore()
    for d in range(NG):
        gg = lax.rem(g + d, NG)
        for ww in ((w,) if d else ()) + (zp, zm, yp, ym, y2):
            pl.semaphore_signal(barrier, inc=1, device_id=(gg, ww), device_id_type=MESH)

    loads[0].wait()
    for k in range(NQ):
        tnat[k:k + 1, :] = trow[:, k * 128:(k + 1) * 128].astype(F32)
    tsend[...] = tnat[...].astype(BF16).reshape(NG, 24, 128)
    pl.semaphore_wait(barrier, 6 * NG - 1)

    for d in range(NG):
        gg = lax.rem(g + d, NG)
        piece = tsend.at[gg]
        if d:
            rcopy(piece, st0.at[g], s0_send, s0_recv, gg, w).start()
        for slot, ww in ((0, yp), (1, ym), (2, y2)):
            rcopy(tsend.at[gg, pl.ds(0, 8)], sty.at[slot, g], sy_send, sy_recv.at[slot], gg, ww).start()
        for slot, ww in ((0, zp), (1, zm)):
            rcopy(tsend.at[gg, pl.ds(8, 16)], stz.at[slot, g], sz_send, sz_recv.at[slot], gg, ww).start()
    st0[g] = tsend[g]

    loads[1].wait()
    qi = lax.broadcasted_iota(jnp.int32, (6, Q), 1) // 64
    onehot = jnp.where(qi == lax.broadcasted_iota(jnp.int32, (6, Q), 0), 1.0, 0.0).astype(F32)
    mask[...] = lax.dot_general(
        fl[...].astype(F32), onehot, (((0,), (0,)), ((), ())), preferred_element_type=F32
    )
    loads[2].wait()

    def screen(i, _):
        m = mask[pl.ds(i, 1), :].astype(BF16)
        rows = pl.ds(pl.multiple_of(i * 64, 64), 64)
        vbuf[rows, :] = vbuf[rows, :] * m
        return 0

    lax.fori_loop(0, 48, screen, 0)

    for c in loads[3:]:
        c.wait()
    i0 = lax.broadcasted_iota(jnp.int32, (64, 64), 0)
    i1 = lax.broadcasted_iota(jnp.int32, (64, 64), 1)
    perm = jnp.where(i1 == lax.rem(i0, 32) * 2 + i0 // 32, 1.0, 0.0).astype(BF16)
    dn = (((1,), (0,)), ((), ()))
    dt = (((1,), (1,)), ((), ()))
    dl = (((0,), (0,)), ((), ()))

    def dot(a, b, d):
        return lax.dot_general(a, b, d, preferred_element_type=F32)

    for t in range(6):
        x = tnat[t * 32:(t + 1) * 32, :]
        xc = jnp.concatenate([x[:, :64], x[:, 64:]], axis=0).astype(BF16)
        f = fbuf[t]
        fh = f.astype(BF16)
        fl_ = (f - fh.astype(F32)).astype(BF16)
        r = rbuf[t]
        rh = r.astype(BF16)
        rl = (r - rh.astype(F32)).astype(BF16)
        c = dot(perm, xc, dl).astype(BF16)
        fph = dot(perm, fh, dn).astype(BF16)
        fpl = dot(perm, fl_, dn).astype(BF16)
        o = dot(fph, c, dn) + dot(fpl, c, dn) + dot(xc, rh, dt) + dot(xc, rl, dt)
        base[t * 32:(t + 1) * 32, :] = jnp.concatenate([o[:32], o[32:]], axis=1)

    inv3[...] = 1.0 / (pls[...] - hls[0])

    def add_exchange(k, _):
        for j in range(8):
            q = k * 8 + j
            o = pl.multiple_of(q * 128, 128)
            base3[q] = base[pl.ds(q, 1), :] + erow[:, pl.ds(o, 128)].astype(F32)
        return 0

    lax.fori_loop(0, NQ // 8, add_exchange, 0)

    def send_a(blk, ww, rs):
        rcopy(ta.at[blk], ta.at[blk], ta_send, rs, g, ww).start()

    def send_b(blk, ww, rs):
        rcopy(tb.at[blk], tb.at[blk], tb_send, rs, g, ww).start()

    def wait_a(blk, rs):
        rcopy(ta.at[blk], ta.at[blk], ta_send, rs, g, w).wait_recv()

    def wait_b(blk, rs):
        rcopy(tb.at[blk], tb.at[blk], tb_send, rs, g, w).wait_recv()

    def pack(staged, n, first, groups, dst, blk):
        scr[0:8 * n, :] = staged.astype(F32).reshape(8 * n, 128)
        for m in range(groups):
            top = scr[pl.ds(first + m, 8, stride=n), :]
            bottom = scr[pl.ds(first + groups + m, 8, stride=n), :]
            dst[blk, :, m * 128:(m + 1) * 128] = jnp.concatenate([top, bottom], axis=0).astype(BF16)

    def col(s, d):
        return z - s if d == 0 else z + s % 8

    rcopy(st0.at[pl.ds(0, 7)], st0.at[pl.ds(0, 7)], s0_send, s0_recv, g, w).wait_recv()
    pack(st0[...], 24, 0, 4, ta, w)
    for d in range(2):
        send_a(w, zn[d], az_recv.at[d, 1, 0])
    pack(st0[...], 24, 8, 8, tb, w)
    send_b(w, yp, by_recv.at[0, 1, 0])
    send_b(w, ym, by_recv.at[0, 1, 1])
    for d in range(2):
        rcopy(stz.at[d], stz.at[d], sz_send, sz_recv.at[d], g, w).wait_recv()
        blk = wid(y, col(1, d))
        pack(stz[d], 16, 0, 8, tb, blk)
        send_b(blk, zn[d], bz_recv.at[d, 2])
        send_b(blk, yp, by_recv.at[1, d, 0])
        send_b(blk, ym, by_recv.at[1, d, 1])
    for slot, dy in ((0, 3), (1, 1), (2, 2)):
        rcopy(sty.at[slot], sty.at[slot], sy_send, sy_recv.at[slot], g, w).wait_recv()
        blk = wid(y + dy, z)
        pack(sty[slot], 8, 0, 4, ta, blk)
        for d in range(2):
            send_a(blk, zn[d], az_recv.at[d, 1, dy])


    def z_b(s):
        for d in range(2):
            last = 8 - d
            if s > last:
                continue
            blk = wid(y, col(s, d))
            wait_b(blk, bz_recv.at[d, s])
            if s < last:
                send_b(blk, zn[d], bz_recv.at[d, s + 1])
            send_b(blk, yp, by_recv.at[s, d, 0])
            send_b(blk, ym, by_recv.at[s, d, 1])
            if s == 8:
                send_b(blk, y2, by_recv.at[s, d, 2])

    def z_a(s, dy):
        for d in range(2):
            last = 8 - d
            if s > last:
                continue
            blk = wid(y + dy, col(s, d))
            wait_a(blk, az_recv.at[d, s, dy])
            if s < last:
                send_a(blk, zn[d], az_recv.at[d, s + 1, dy])

    def y_b(s):
        if 1 <= s <= 7:
            blk = wid(y - 1, col(s, 0))
            wait_b(blk, by_recv.at[s, 0, 0])
            send_b(blk, yp, by_recv.at[s, 0, 2])
        if 0 <= s <= 7:
            blk = wid(y + 1, col(s, 1))
            wait_b(blk, by_recv.at[s, 1, 1])
            send_b(blk, ym, by_recv.at[s, 1, 2])

    def blocks(s):
        return [wid(y + dy, col(s, d)) for d in range(2) for dy in range(NY)]

    def half(o, h):
        return o.reshape(8, 16, Q)[:, 8 * h:8 * h + 8, :].reshape(64, Q)

    def comp_a(s):
        x = jnp.concatenate([ta[b] for b in blocks(s)], axis=0)
        o0 = jnp.dot(x, vbuf[0:KA, :], preferred_element_type=F32)
        o1 = jnp.dot(x, vbuf[KA:2 * KA, :], preferred_element_type=F32)
        acc[...] = half(o0, 0) + half(o1, 1)

    def comp_b(s, h):
        if h == 0:
            if s == 8:
                wait_b(wid(y - 1, col(s, 0)), by_recv.at[s, 0, 0])
            wait_b(wid(y + 1, col(s, 0)), by_recv.at[s, 0, 1])
            wait_b(wid(y + 2, col(s, 0)), by_recv.at[s, 0, 2])
            wait_b(wid(y - 1, col(s, 1)), by_recv.at[s % 8, 1, 0])
            wait_b(wid(y + 2, col(s, 1)), by_recv.at[s % 8, 1, 2])
        x = jnp.concatenate([tb[b] for b in blocks(s)], axis=0)
        k0 = 2 * KA + h * KB
        o = half(jnp.dot(x, vbuf[k0:k0 + KB, :], preferred_element_type=F32), h) + acc[...]
        if h == 0:
            acc[...] = o
            return
        for c in range(3):
            obuf[c] = o[:, c * 128:(c + 1) * 128]
        j = (s - 1) * NG
        for d in range(NG):
            for c in range(3):
                sbuf[j + d, :, c * 128:(c + 1) * 128] = obuf[c, pl.ds(d, 8, stride=8), :]
        for d in range(1, NG):
            gg = lax.rem(g + d, NG)
            rcopy(sbuf.at[j + gg], xr.at[j + g], x_send, x_recv.at[s - 1], gg, w).start()
        xr[j + g] = sbuf[j + g]

    def reduce(s):
        j = (s - 1) * NG
        win = pl.ds(j, NG - 1)
        rcopy(sbuf.at[win], xr.at[win], x_send, x_recv.at[s - 1], g, w).wait_recv()
        tot = jnp.sum(xr[j:j + NG], axis=0)
        for n in range(8):
            for c in range(3):
                fs[(s - 1) * 24 + 3 * n + c] = tot[n:n + 1, c * 128:(c + 1) * 128]
        for d in range(2):
            for dy in (2, 1, 3, 0):
                n = d * NY + dy
                f0 = (s - 1) * 24 + 3 * n
                if s == 8 and d == 1 and dy == 0:
                    for c in range(3):
                        lad[3 * w + c] = fs[f0 + c]
                else:
                    rcopy(
                        fs.at[pl.ds(f0, 3)], lad.at[pl.ds(3 * w, 3)], l_send, l_recv, g, wid(y + dy, col(s, d))
                    ).start()

    for i in range(1, 9):
        z_b(i + 1)
        if i > 1:
            comp_a(i - 1)
        if i == 1:
            y_b(0)
        y_b(i)
        z_a(i, 0)
        if i > 1:
            comp_b(i - 1, 0)
        z_a(i, 3)
        if i > 1:
            comp_b(i - 1, 1)
        z_a(i, 1)
        if i > 2:
            reduce(i - 2)
        z_a(i, 2)
    comp_a(8)
    comp_b(8, 0)
    comp_b(8, 1)
    reduce(7)
    reduce(8)

    part = pl.ds(0, 3 * (NW - 1))
    rcopy(fs.at[part], lad.at[part], l_send, l_recv, g, w).wait_recv()
    out[...] = (lad[...] + base3[...]) * inv3[...]

    rcopy(st0.at[pl.ds(0, 7)], st0.at[pl.ds(0, 7)], s0_send, s0_recv, g, w).wait_send()
    rcopy(stz, stz, sz_send, s0_recv, g, w).wait_send()
    rcopy(sty, sty, sy_send, s0_recv, g, w).wait_send()
    rcopy(ta.at[pl.ds(0, 60)], ta.at[pl.ds(0, 60)], ta_send, s0_recv, g, w).wait_send()
    rcopy(tb.at[pl.ds(0, 61)], tb.at[pl.ds(0, 61)], tb_send, s0_recv, g, w).wait_send()
    rcopy(sbuf.at[pl.ds(0, 56)], xr.at[pl.ds(0, 56)], x_send, x_recv.at[0], g, w).wait_send()
    rcopy(fs.at[part], lad.at[part], l_send, l_recv, g, w).wait_send()


def local(t, e, v, flags, f, r, hls, pls):
    any_spec = pl.BlockSpec(memory_space=pl.ANY)
    vm = pltpu.VMEM
    dma = pltpu.SemaphoreType.DMA
    res = pl.pallas_call(
        kernel,
        out_shape=jax.ShapeDtypeStruct((NQ, 1, 128), F32),
        in_specs=[any_spec] * 6 + [pl.BlockSpec(memory_space=pltpu.SMEM), any_spec],
        out_specs=pl.BlockSpec(memory_space=pltpu.VMEM),
        scratch_shapes=[
            vm((1, 24576), BF16),
            vm((1, 24576), BF16),
            vm((KG, Q), BF16),
            vm((6, 48), jnp.int32),
            vm((48, Q), F32),
            vm((6, 64, 64), F32),
            vm((6, 64, 64), F32),
            vm((NQ, 1, 128), F32),
            vm((NQ, 128), F32),
            vm((NQ, 128), F32),
            vm((NQ, 1, 128), F32),
            vm((NQ, 1, 128), F32),
            vm((NG, 24, 128), BF16),
            vm((NG, 24, 128), BF16),
            vm((2, NG, 16, 128), BF16),
            vm((3, NG, 8, 128), BF16),
            vm((NQ, 128), F32),
            vm((NW, 16, KA), BF16),
            vm((NW, 16, KB), BF16),
            vm((64, Q), F32),
            vm((3, 64, 128), F32),
            vm((64, 8, Q), F32),
            vm((64, 8, Q), F32),
            vm((NQ, 1, 128), F32),
            vm((NQ, 1, 128), F32),
            dma((7,)),
            dma,
            dma((2,)),
            dma((3,)),
            dma((2, 9, 4)),
            dma((2, 9)),
            dma((9, 2, 3)),
            dma((8,)),
            dma,
            dma,
            dma,
            dma,
            dma,
            dma,
            dma,
            dma,
        ],
        compiler_params=pltpu.CompilerParams(
            collective_id=0, has_side_effects=True, vmem_limit_bytes=60 * 1024 * 1024
        ),
        name="ladder",
    )(t, e, v, flags.T, f, r, hls, pls.reshape(NQ, 1, 128))
    return res.reshape(1, 24576)


def solution(mesh):
    return jax.shard_map(
        local,
        mesh=mesh,
        in_specs=(
            P(("grp", "wide"), None),
            P(("grp", "wide"), None),
            P("grp", "wide"),
            P("grp", "wide"),
            P(),
            P(),
            P(("grp", "wide")),
            P(),
        ),
        out_specs=P(("grp", "wide"), None),
        check_vma=False,
    )
```

time: 307 us -> 66.6 us (0.22)
  waiting for transfers between devices: 229 us -> 0 us
  Pallas kernels: 0 us -> 64.2 us
  starting transfers between devices: 27.5 us -> 0 us
  other arithmetic: 22.8 us -> 0 us
  between operations: 14.2 us -> 0.66 us
  local copies, waits for them, and re-layouts: 6.77 us -> 1.54 us
  matrix products: 4.61 us -> 0 us
    all_gather x1 -> x0, waiting for transfers between devices: 151 us -> none  [local(): gathered = lax.all_gather(cluster_coefficients, 'wide', axis=0, tiled=True)]
    pallas_call x0 -> x1, Pallas kernels: none -> 64.2 us  [local(): pl.pallas_call(kernel, out_shape=jax.ShapeDtypeStruct((NQ, 1, 128), F32),...]
    all_to_all x2 -> x0, waiting for transfers between devices: 47.4 us -> none  [the longest x1 33.7 us: local(): lax.all_to_all(gathered, 'grp', split_axis=1, concat_axis=0, tiled=True)]
    unnamed x3 -> x0, waiting for transfers between devices: 30.6 us -> none
    all_to_all x2 -> x0, starting transfers between devices: 27.5 us -> none  [the longest x1 14.4 us: local(): lax.all_to_all(summed, 'wide', split_axis=0, concat_axis=1, tiled=True)]
    all_gather x1 -> x0, other arithmetic: 18.3 us -> none  [local(): gathered = lax.all_gather(cluster_coefficients, 'wide', axis=0, tiled=True)]
    dot_general x3 -> x0, matrix products: 4.61 us -> none  [the longest x1 4 us: local(): jnp.dot(regrouped, pruned_particle_contraction, preferred_element_type=jn...]
    mul x1 -> x0, other arithmetic: 3.37 us -> none  [prune_submatrix(): return (shaped * kept_column_flags[:, None, :]).reshape(cd_rows, ab_cols)]
  transfers between devices with their start and end apart: 4 -> 0, of which waited for: 4 -> 0; matrix products, arithmetic and copies ran while one was open for 2% -> 0% of each run, Pallas kernels for 0% -> 0%
where the time goes in v2:
time: 66.6 us; the launch traced here: 66.4 us
  Pallas kernels  64.2 us (96%)
  local copies, waits for them, and re-layouts  1.54 us (2%)
    pallas_call x1, Pallas kernels, local(): pl.pallas_call(kernel, out_shape=jax.ShapeDtypeStruct((NQ, 1, 128), F32),...  64.2 us
    unnamed x1, local copies, waits for them, and re-layouts  1.54 us

profile of v2, /device:TPU:1, one launch (start us, length us, event | category | flops | bytes accessed | tf_op | source)
XLA Modules:
  0.0 66.4 jit_solution(15862244720916737785)
XLA Ops:
  0.7 64.2 %ladder.1 = f32[192,1,128]{2,1,0:T(1,128)} custom-call(bf16[1,24576]{1,0:T(2,128)(2,1)} %t_hbm.1, bf16[1,24576]{1,0:T(2,128)(2,1)} %e_hbm.1, bf16[3072,384]{1,0:T(8,128)(2,1)} %v_hbm.1, s32[6,48]{1,0:T(8,128)} %bitcast.5, f32[6,64,64]{2,1,0:T(8,128)} %f_hbm.1, f32[6,64,64]{2,1,0:T(8,128)} %r_hbm.1, f32[1]{0:T(128)S(6)} %copy.10.hls, f32[192,1,128]{2,1,0:T(1,128)} %bitcast.4), custom_call_target="tpu_custom_call" | custom-call | tf_op jit(solution)/shard_map/ladder/pallas_call | solution.py:311
  64.9 1.5 %copy.11 = f32[1,24576]{1,0:T(1,128)} copy(f32[1,24576]{1,0:T(1,128)} %bitcast.3) | data formatting | bytes 196608
